TPU v7x, 32 devices: a whole 2x2x4 slice. The times are simulated.
32 devices in a mesh: pairs: 8 (over y, x, core), aux: 4 (over z).
Axes of the slice: x: 2, y: 2, z: 4, core: 2. Of those that a mesh axis runs over, the one named last changes fastest.
Arguments:
- panels: bfloat16 [64, 3584, 256], P(None, ('pairs', 'aux')), may hold values from -0.59765625 to 0.59765625
- domain: int32 [8, 6], replicated, may hold values from 0 to 63, as said below
- pair_slots: int32 [96, 2], P('pairs'), may hold values from 0 to 5
- ranks: int32 [96, 2], P('pairs'), may hold values from 40 to 128
- transforms: bfloat16 [96, 2, 256, 128], P('pairs'), may hold values from -0.375 to 0.375
- trial: bfloat16 [96, 2, 128, 128], P('pairs'), may hold values from -0.5 to 0.5
Outputs:
- sigma: bfloat16 [96, 2, 128, 128], P('pairs', None, 'aux')
Inputs may be any that keep to these rules, and one draw needn't show every extreme that they name: `domain`: each row holds 6 different LMO numbers.
All inputs are finite; a program needn't handle non-finite values.
Results may differ from a plain program's by a relative error of at most 0.0039.
Values may be sent and summed in bfloat16 or wider, within the bound.
A program may use at most 128 MiB of HBM per device.

v0:
```python
import functools

import jax
import jax.numpy as jnp
from jax import lax
from jax.experimental import pallas as pl
from jax.experimental.pallas import tpu as pltpu
from jax.sharding import PartitionSpec as P

MESH = pl.DeviceIdType.MESH
CHUNKS = 4


def peer_of(me, offset, count):
    if count & (count - 1):
        return lax.rem(me + offset, count)
    peer = me
    bit = 1
    while bit < count:
        if offset & bit:
            peer = peer + bit * (1 - 2 * lax.rem(me // bit, 2))
        bit *= 2
    return peer


def fused_kernel(
    n, m, plan, domain_ref, slots_ref, ranks_ref, panels_ref, d_ref, c_ref, out_ref,
    panels, outgoing, d_raw, d_mask, c_raw, acc, send_buf, landed,
    local_sem, send_sem, recv_sem, part_send, part_recv, *received,
):
    me = lax.axis_index("pairs")
    mine = lax.axis_index("aux")
    pairs, roots, nv, width = d_ref.shape
    slots = received[0].shape[0]
    rows = received[0].shape[2]
    strip = width // m
    group = pairs // CHUNKS

    barrier = pltpu.get_barrier_semaphore()
    for offset in range(1, n):
        pl.semaphore_signal(barrier, inc=1, device_id=(peer_of(me, offset, n), mine), device_id_type=MESH)
    for offset in range(1, m):
        pl.semaphore_signal(barrier, inc=1, device_id=(me, lax.rem(mine + offset, m)), device_id_type=MESH)
    panels_copy = pltpu.make_async_copy(panels_ref, panels, local_sem.at[0])
    panels_copy.start()
    d_copy = pltpu.make_async_copy(d_ref, d_raw, local_sem.at[1])
    d_copy.start()
    c_copy = pltpu.make_async_copy(c_ref, c_raw, local_sem.at[2])
    c_copy.start()
    pl.semaphore_wait(barrier, n + m - 2)

    panels_copy.wait()
    place = {offset: (stage, lane) for stage, group in enumerate(plan) for lane, offset in enumerate(group)}
    copies = {}
    for offset in range(1, n):
        peer = peer_of(me, offset, n)
        for slot in range(slots):
            outgoing[offset - 1, slot] = panels[domain_ref[peer, slot]]
        stage, lane = place[offset]
        copies[offset] = pltpu.make_async_remote_copy(
            src_ref=outgoing.at[offset - 1],
            dst_ref=received[stage].at[:, lane],
            send_sem=send_sem.at[offset],
            recv_sem=recv_sem.at[offset],
            device_id=(peer, mine),
            device_id_type=MESH,
        )
        if offset > 1:
            copies[offset - 1].start()
    for slot in range(slots):
        received[0][slot, 0] = panels[domain_ref[me, slot]]
    copies[n - 1].start()

    columns = lax.broadcasted_iota(jnp.int32, (1, width), 1)
    row_ids = lax.broadcasted_iota(jnp.int32, (width, 1), 0)
    d_copy.wait()
    c_copy.wait()

    def mask_pair(pair, carry):
        for root in range(roots):
            rank = ranks_ref[root, pair]
            d_mask[pair, :, root * width:(root + 1) * width] = jnp.where(
                columns < rank, d_raw[pair, root], jnp.zeros((), d_raw.dtype)
            )
            keep = (columns < rank) & (row_ids < rank)
            c_raw[pair, root] = jnp.where(keep, c_raw[pair, root], jnp.zeros((), c_raw.dtype))
        return carry

    lax.fori_loop(0, pairs, mask_pair, 0)

    def partial_of(pair, block):
        both = block.shape[1] * rows
        left = block[slots_ref[0, pair]].reshape(both, nv)
        right = block[slots_ref[1, pair]].reshape(both, nv)
        coeffs = d_mask[pair]
        left = jnp.dot(left, coeffs, preferred_element_type=jnp.float32).astype(jnp.bfloat16)
        right = jnp.dot(right, coeffs, preferred_element_type=jnp.float32).astype(jnp.bfloat16)
        return [
            lax.dot_general(
                left[:, root * width:(root + 1) * width],
                right[:, root * width:(root + 1) * width],
                (((0,), (0,)), ((), ())),
                preferred_element_type=jnp.float32,
            )
            for root in range(roots)
        ]

    stages = len(received)
    for stage in range(stages):
        for offset in plan[stage]:
            if offset:
                copies[offset].wait_recv()
        block = received[stage]
        if stage < stages - 1:

            def accumulate(pair, carry, block=block, stage=stage):
                parts = partial_of(pair, block)
                for root in range(roots):
                    if stage == 0:
                        acc[pair, root] = parts[root]
                    else:
                        acc[pair, root] += parts[root]
                return carry

            lax.fori_loop(0, pairs, accumulate, 0, unroll=2)

    block = received[stages - 1]

    def finish(pair, carry):
        parts = partial_of(pair, block)
        for root in range(roots):
            kmat = parts[root] if stages == 1 else acc[pair, root] + parts[root]
            rounded = kmat.astype(jnp.bfloat16)
            amplitude = c_raw[pair, root]
            with_right = jnp.dot(rounded, amplitude, preferred_element_type=jnp.float32)
            with_left = lax.dot_general(
                amplitude, rounded, (((1,), (1,)), ((), ())), preferred_element_type=jnp.float32
            )
            sigma = kmat + with_right + with_left
            acc[pair, root] = sigma
            for owner in range(m):
                send_buf[owner, pair, root] = sigma[owner * strip:(owner + 1) * strip].astype(jnp.bfloat16)
        return carry

    sums = []
    for chunk in range(CHUNKS):
        lax.fori_loop(chunk * group, (chunk + 1) * group, finish, 0, unroll=group)
        for offset in range(1, m):
            peer = lax.rem(mine + offset, m)
            copy = pltpu.make_async_remote_copy(
                src_ref=send_buf.at[peer, pl.ds(chunk * group, group)],
                dst_ref=landed.at[offset - 1, pl.ds(chunk * group, group)],
                send_sem=part_send.at[chunk, offset],
                recv_sem=part_recv.at[chunk, offset],
                device_id=(me, peer),
                device_id_type=MESH,
            )
            copy.start()
            sums.append((chunk, offset, copy))

    for chunk in range(CHUNKS):
        for at, offset, copy in sums:
            if at == chunk:
                copy.wait_recv()
        part = pl.ds(chunk * group, group)
        total = acc[part, :, pl.ds(mine * strip, strip), :]
        for offset in range(1, m):
            total = total + landed[offset - 1, part].astype(jnp.float32)
        out_ref[part] = total.astype(out_ref.dtype)
    for copy in copies.values():
        copy.wait_send()
    for _, _, copy in sums:
        copy.wait_send()


def per_device(n, m, panels, domain, pair_slots, ranks, transforms, trial):
    pairs, roots, nv, width = transforms.shape
    slots = domain.shape[1]
    rows = panels.shape[1]
    plan = [(offset, offset + 1) for offset in range(0, n - 2, 2)] + [(n - 2,), (n - 1,)]
    smem = pl.BlockSpec(memory_space=pltpu.SMEM)
    hbm = pl.BlockSpec(memory_space=pltpu.HBM)
    return pl.pallas_call(
        functools.partial(fused_kernel, n, m, plan),
        in_specs=[smem, smem, smem, hbm, hbm, hbm],
        out_specs=pl.BlockSpec(memory_space=pltpu.VMEM),
        out_shape=jax.ShapeDtypeStruct((pairs, roots, width // m, width), jnp.bfloat16),
        scratch_shapes=[
            pltpu.VMEM(panels.shape, panels.dtype),
            pltpu.VMEM((n - 1, slots, rows, nv), panels.dtype),
            pltpu.VMEM((pairs, roots, nv, width), transforms.dtype),
            pltpu.VMEM((pairs, nv, roots * width), transforms.dtype),
            pltpu.VMEM((pairs, roots, width, width), trial.dtype),
            pltpu.VMEM((pairs, roots, width, width), jnp.float32),
            pltpu.VMEM((m, pairs, roots, width // m, width), jnp.bfloat16),
            pltpu.VMEM((m - 1, pairs, roots, width // m, width), jnp.bfloat16),
            pltpu.SemaphoreType.DMA((3,)),
            pltpu.SemaphoreType.DMA((n,)),
            pltpu.SemaphoreType.DMA((n,)),
            pltpu.SemaphoreType.DMA((CHUNKS, m)),
            pltpu.SemaphoreType.DMA((CHUNKS, m)),
        ]
        + [pltpu.VMEM((slots, len(group), rows, nv), panels.dtype) for group in plan],
        compiler_params=pltpu.CompilerParams(
            collective_id=0, has_side_effects=True, vmem_limit_bytes=60 * 2**20
        ),
    )(domain, pair_slots.T, ranks.T, panels, transforms, trial)


def solution(mesh):
    return jax.shard_map(
        functools.partial(per_device, mesh.shape["pairs"], mesh.shape["aux"]),
        mesh=mesh,
        in_specs=(
            P(None, ("pairs", "aux"), None),
            P(),
            P("pairs", None),
            P("pairs", None),
            P("pairs", None, None, None),
            P("pairs", None, None, None),
        ),
        out_specs=P("pairs", None, "aux", None),
        check_vma=False,
    )
```

profile of v0, /device:TPU:1, one launch (start us, length us, event | category | flops | bytes accessed | tf_op | source)
XLA Modules:
  0.0 59.9 jit_solution(6878251924854711098)
XLA Ops:
  0.0 58.3 %shard_map.64 = bf16[12,2,32,128]{3,2,1,0:T(8,128)(2,1)} custom-call(s32[8,6]{1,0:T(8,128)} %domain_ref.1, s32[2,12]{1,0:T(2,128)} %bitcast.2, s32[2,12]{1,0:T(2,128)} %bitcast.3, bf16[64,112,256]{2,1,0:T(8,128)(2,1)} %panels_ref.1, bf16[12,2,256,128]{3,2,1,0:T(8,128)(2,1)} %d_ref.1, bf16[12,2,128,128]{3,2,1,0:T(8,128)(2,1)} %c_ref.1), custom_call_target="tpu_custom_call" | custom-call | tf_op jit(solution)/shard_map/pallas_call | solution.py:183
  58.3 1.6 %copy.8 = bf16[12,2,32,128]{3,2,1,0:T(8,128)(2,1)} copy(bf16[12,2,32,128]{3,2,1,0:T(8,128)(2,1)} %shard_map.64) | data formatting | bytes 393216
where the time goes:
time: 60.5 us; the launch traced here: 59.9 us
  Pallas kernels  58.3 us (96%)
  local copies, waits for them, and re-layouts  1.62 us (3%)
    pallas_call x1, Pallas kernels, per_device(): pl.pallas_call(functools.partial(fused_kernel, n, m, plan), in_specs=[sme...  58.3 us
    unnamed x1, local copies, waits for them, and re-layouts  1.62 us

commit v1 on v0

v1 whole, which is shorter than its diff:
```python
import functools

import jax
import jax.numpy as jnp
from jax import lax
from jax.experimental import pallas as pl
from jax.experimental.pallas import tpu as pltpu
from jax.sharding import PartitionSpec as P

MESH = pl.DeviceIdType.MESH
CORES = 2


def peer_of(me, offset, count):
    if count & (count - 1):
        return lax.rem(me + offset, count)
    peer = me
    bit = 1
    while bit < count:
        if offset & bit:
            peer = peer + bit * (1 - 2 * lax.rem(me // bit, 2))
        bit *= 2
    return peer


def complete_after(slots, pairs):
    sure = pairs
    counts = [pairs]
    for left in range(slots, 1, -1):
        sure -= min(sure, 2 * sure // left)
        counts.insert(0, sure)
    return counts


def elimination(slots_ref, slots, pairs):
    bits = (pairs + 1).bit_length()
    left = [slots_ref[0, pair] for pair in range(pairs)]
    right = [slots_ref[1, pair] for pair in range(pairs)]
    fields = 31 // bits
    words = -(-slots // fields)

    def mark(slot, word):
        low = word * fields
        shift = slot - low
        inside = (shift >= 0) & (shift < fields)
        return jnp.where(inside, jnp.left_shift(1, jnp.where(inside, shift, 0) * bits), 0)

    marks = [[mark(left[p], w) | mark(right[p], w) for w in range(words)] for p in range(pairs)]
    alive = [jnp.int32(1)] * pairs
    rank = [jnp.int32(0)] * pairs
    place = [jnp.int32(0)] * slots
    taken = [jnp.int32(0)] * slots
    for spot in range(slots - 1, -1, -1):
        totals = [sum(alive[p] * marks[p][w] for p in range(pairs)) for w in range(words)]
        best, pick = None, None
        for slot in range(slots):
            count = (totals[slot // fields] >> (bits * (slot % fields))) & (2**bits - 1)
            count = count + taken[slot] * 2**bits
            if best is None:
                best, pick = count, jnp.int32(slot)
            else:
                less = count < best
                best = jnp.where(less, count, best)
                pick = jnp.where(less, slot, pick)
        for slot in range(slots):
            hit = pick == slot
            place[slot] = jnp.where(hit, spot, place[slot])
            taken[slot] = jnp.where(hit, 1, taken[slot])
        gone = []
        for p in range(pairs):
            touch = (left[p] == pick) | (right[p] == pick)
            gone.append(jnp.where(touch, alive[p], 0))
            alive[p] = alive[p] - gone[p]
        at = sum(alive)
        for p in range(pairs):
            rank[p] = jnp.where(gone[p] == 1, at, rank[p])
            at = at + gone[p]
    return place, rank


def fused_kernel(
    n, m, domain_ref, slots_ref, ranks_ref, panels_ref, d_ref, c_ref, out_ref,
    panels, outgoing, recv, block, d_raw, d_mask, c_raw, acc, send_buf, landed, total,
    place_ref, rank_ref, perm_ref, mine_order, orders,
    local_sem, send_sem, recv_sem, order_send, order_recv, part_send, part_recv,
):
    me = lax.axis_index("pairs")
    mine = lax.axis_index("aux")
    core = lax.rem(me, CORES)
    chip = me // CORES
    chips = n // CORES
    pairs, roots, nv, width = d_ref.shape
    slots = domain_ref.shape[1]
    rows = panels_ref.shape[1]
    strip = width // m
    sure = complete_after(slots, pairs)
    last = CORES - 1

    def device(k, dest):
        return peer_of(chip, k, chips) * CORES + dest

    barrier = pltpu.get_barrier_semaphore()
    for k in range(chips):
        for dest in range(CORES):
            if k:
                pl.semaphore_signal(barrier, inc=1, device_id=(device(k, dest), mine), device_id_type=MESH)
    pl.semaphore_signal(barrier, inc=1, device_id=(chip * CORES + 1 - core, mine), device_id_type=MESH)
    for offset in range(1, m):
        pl.semaphore_signal(barrier, inc=1, device_id=(me, lax.rem(mine + offset, m)), device_id_type=MESH)
    panels_copy = pltpu.make_async_copy(panels_ref, panels, local_sem.at[0])
    panels_copy.start()
    d_copy = pltpu.make_async_copy(d_ref, d_raw, local_sem.at[1])
    d_copy.start()
    c_copy = pltpu.make_async_copy(c_ref, c_raw, local_sem.at[2])
    c_copy.start()

    place, rank = elimination(slots_ref, slots, pairs)
    for slot in range(slots):
        place_ref[slot] = jnp.where(core == last, place[slot], slot)
    for pair in range(pairs):
        rank_ref[pair] = rank[pair]
    for spot in range(slots):
        chosen = sum(jnp.where(place[slot] == spot, slot, 0) for slot in range(slots))
        mine_order[0, spot] = jnp.where(core == last, chosen, spot)
    for q in range(pairs):
        perm_ref[q] = sum(jnp.where(rank[pair] == q, pair, 0) for pair in range(pairs))

    pl.semaphore_wait(barrier, n + m - 2)

    def order_copy(peer, k, slot):
        return pltpu.make_async_remote_copy(
            src_ref=mine_order,
            dst_ref=orders.at[slot],
            send_sem=order_send.at[k],
            recv_sem=order_recv.at[slot],
            device_id=(peer, mine),
            device_id_type=MESH,
        )

    @pl.when(core == last)
    def _():
        for k in range(1, chips):
            for dest in range(CORES):
                order_copy(device(k, dest), k * CORES + dest, chip).start()
        order_copy(chip * CORES, 0, chip).start()

    panels_copy.wait()

    def panel_copy(k, dest, spot):
        return pltpu.make_async_remote_copy(
            src_ref=outgoing.at[dest, k, spot],
            dst_ref=recv.at[spot, k * CORES + core],
            send_sem=send_sem.at[dest, k, spot],
            recv_sem=recv_sem.at[spot, k * CORES + core],
            device_id=(device(k, dest), mine),
            device_id_type=MESH,
        )

    def send_all(dest, slot_of):
        waiting = None
        for spot in range(slots):
            for k in range(1, chips):
                peer = device(k, dest)
                outgoing[dest, k, spot] = panels[domain_ref[peer, slot_of(k, spot)]]
                if waiting is not None:
                    waiting.start()
                waiting = panel_copy(k, dest, spot)
        peer = chip * CORES + dest
        for spot in range(slots):
            outgoing[dest, 0, spot] = panels[domain_ref[peer, slot_of(0, spot)]]
        waiting.start()

        @pl.when(core != dest)
        def _():
            for spot in range(slots):
                panel_copy(0, dest, spot).start()

        @pl.when(core == dest)
        def _():
            for spot in range(slots):
                recv[spot, dest] = outgoing[dest, 0, spot]

    for dest in range(last):
        send_all(dest, lambda k, spot: spot)

    for k in range(1, chips):
        slot = peer_of(chip, k, chips)
        order_copy(chip * CORES, 0, slot).wait_recv()

    @pl.when(core != last)
    def _():
        order_copy(chip * CORES, 0, chip).wait_recv()

    @pl.when(core == last)
    def _():
        for spot in range(slots):
            orders[chip, 0, spot] = mine_order[0, spot]

    send_all(last, lambda k, spot: orders[peer_of(chip, k, chips), 0, spot])

    columns = lax.broadcasted_iota(jnp.int32, (1, width), 1)
    row_ids = lax.broadcasted_iota(jnp.int32, (width, 1), 0)
    d_copy.wait()
    c_copy.wait()

    def mask_pair(pair, carry):
        for root in range(roots):
            limit = ranks_ref[root, pair]
            d_mask[pair, :, root * width:(root + 1) * width] = jnp.where(
                columns < limit, d_raw[pair, root], jnp.zeros((), d_raw.dtype)
            )
            keep = (columns < limit) & (row_ids < limit)
            c_raw[pair, root] = jnp.where(keep, c_raw[pair, root], jnp.zeros((), c_raw.dtype))
        return carry

    lax.fori_loop(0, pairs, mask_pair, 0)

    def part_copy(q, offset):
        peer = lax.rem(mine + offset, m)
        return pltpu.make_async_remote_copy(
            src_ref=send_buf.at[peer, q],
            dst_ref=landed.at[offset - 1, q],
            send_sem=part_send.at[q, offset],
            recv_sem=part_recv.at[q, offset],
            device_id=(me, peer),
            device_id_type=MESH,
        )

    def compute(q, carry):
        pair = perm_ref[q]
        coeffs = d_mask[pair]
        left = block[place_ref[slots_ref[0, pair]]]
        right = block[place_ref[slots_ref[1, pair]]]
        left = jnp.dot(left, coeffs, preferred_element_type=jnp.float32).astype(jnp.bfloat16)
        right = jnp.dot(right, coeffs, preferred_element_type=jnp.float32).astype(jnp.bfloat16)
        for root in range(roots):
            kmat = lax.dot_general(
                left[:, root * width:(root + 1) * width],
                right[:, root * width:(root + 1) * width],
                (((0,), (0,)), ((), ())),
                preferred_element_type=jnp.float32,
            )
            rounded = kmat.astype(jnp.bfloat16)
            amplitude = c_raw[pair, root]
            with_right = jnp.dot(rounded, amplitude, preferred_element_type=jnp.float32)
            with_left = lax.dot_general(
                amplitude, rounded, (((1,), (1,)), ((), ())), preferred_element_type=jnp.float32
            )
            sigma = kmat + with_right + with_left
            acc[q, root] = sigma
            for owner in range(m):
                send_buf[owner, q, root] = sigma[owner * strip:(owner + 1) * strip].astype(jnp.bfloat16)
        for offset in range(1, m):
            part_copy(q, offset).start()
        return carry

    def take(spot):
        for lane in range(n):
            if lane < CORES:

                @pl.when(core != lane)
                def _():
                    arrived(lane, spot).wait_recv()

            else:
                arrived(lane, spot).wait_recv()
        block[spot] = recv[spot].reshape(n * rows, nv)

    def arrived(lane, spot):
        return pltpu.make_async_remote_copy(
            src_ref=outgoing.at[0, 0, spot],
            dst_ref=recv.at[spot, lane],
            send_sem=send_sem.at[0, 0, spot],
            recv_sem=recv_sem.at[spot, lane],
            device_id=(chip * CORES + 1 - core, mine),
            device_id_type=MESH,
        )

    @pl.when(core != last)
    def _():
        for spot in range(slots):
            take(spot)

    done = 0
    for spot in range(slots):

        @pl.when(core == last)
        def _():
            take(spot)

        if sure[spot] > done:
            lax.fori_loop(done, sure[spot], compute, 0)
            done = sure[spot]

    for q in range(pairs):
        for offset in range(1, m):
            part_copy(q, offset).wait_recv()
        value = acc[q, :, pl.ds(pl.multiple_of(mine * strip, strip), strip), :]
        for offset in range(1, m):
            value = value + landed[offset - 1, q].astype(jnp.float32)
        total[q] = value.astype(total.dtype)
    for pair in range(pairs):
        out_ref[pair] = total[rank_ref[pair]]

    for dest in range(CORES):
        for spot in range(slots):
            for k in range(1, chips):
                panel_copy(k, dest, spot).wait_send()

        @pl.when(core != dest)
        def _():
            for spot in range(slots):
                panel_copy(0, dest, spot).wait_send()

    @pl.when(core == last)
    def _():
        for k in range(1, chips):
            for dest in range(CORES):
                order_copy(device(k, dest), k * CORES + dest, chip).wait_send()
        order_copy(chip * CORES, 0, chip).wait_send()

    for q in range(pairs):
        for offset in range(1, m):
            part_copy(q, offset).wait_send()


def per_device(n, m, panels, domain, pair_slots, ranks, transforms, trial):
    pairs, roots, nv, width = transforms.shape
    slots = domain.shape[1]
    rows = panels.shape[1]
    chips = n // CORES
    strip = width // m
    bf16 = jnp.bfloat16
    smem = pl.BlockSpec(memory_space=pltpu.SMEM)
    hbm = pl.BlockSpec(memory_space=pltpu.HBM)
    dma = pltpu.SemaphoreType.DMA
    return pl.pallas_call(
        functools.partial(fused_kernel, n, m),
        in_specs=[smem, smem, smem, hbm, hbm, hbm],
        out_specs=pl.BlockSpec(memory_space=pltpu.VMEM),
        out_shape=jax.ShapeDtypeStruct((pairs, roots, strip, width), bf16),
        scratch_shapes=[
            pltpu.VMEM(panels.shape, bf16),
            pltpu.VMEM((CORES, chips, slots, rows, nv), bf16),
            pltpu.VMEM((slots, n, rows, nv), bf16),
            pltpu.VMEM((slots, n * rows, nv), bf16),
            pltpu.VMEM((pairs, roots, nv, width), bf16),
            pltpu.VMEM((pairs, nv, roots * width), bf16),
            pltpu.VMEM((pairs, roots, width, width), bf16),
            pltpu.VMEM((pairs, roots, width, width), jnp.float32),
            pltpu.VMEM((m, pairs, roots, strip, width), bf16),
            pltpu.VMEM((m - 1, pairs, roots, strip, width), bf16),
            pltpu.VMEM((pairs, roots, strip, width), bf16),
            pltpu.SMEM((slots,), jnp.int32),
            pltpu.SMEM((pairs,), jnp.int32),
            pltpu.SMEM((pairs,), jnp.int32),
            pltpu.SMEM((1, 128), jnp.int32),
            pltpu.SMEM((chips, 1, 128), jnp.int32),
            dma((3,)),
            dma((CORES, chips, slots)),
            dma((slots, n)),
            dma((n,)),
            dma((chips,)),
            dma((pairs, m)),
            dma((pairs, m)),
        ],
        compiler_params=pltpu.CompilerParams(
            collective_id=0, has_side_effects=True, vmem_limit_bytes=60 * 2**20
        ),
    )(domain, pair_slots.T, ranks.T, panels, transforms, trial)


def solution(mesh):
    return jax.shard_map(
        functools.partial(per_device, mesh.shape["pairs"], mesh.shape["aux"]),
        mesh=mesh,
        in_specs=(
            P(None, ("pairs", "aux"), None),
            P(),
            P("pairs", None),
            P("pairs", None),
            P("pairs", None, None, None),
            P("pairs", None, None, None),
        ),
        out_specs=P("pairs", None, "aux", None),
        check_vma=False,
    )
```

time: 60.5 us -> 50.6 us (0.84)
  Pallas kernels: 58.3 us -> 48.8 us
    pallas_call x1, Pallas kernels: 58.3 us -> 48.8 us  [per_device(): pl.pallas_call(functools.partial(fused_kernel, n, m), in_specs=[smem, sme...]
where the time goes in v1:
time: 50.6 us; the launch traced here: 50.4 us
  Pallas kernels  48.8 us (96%)
  local copies, waits for them, and re-layouts  1.62 us (3%)
    pallas_call x1, Pallas kernels, per_device(): pl.pallas_call(functools.partial(fused_kernel, n, m), in_specs=[smem, sme...  48.8 us
    unnamed x1, local copies, waits for them, and re-layouts  1.62 us

profile of v1, /device:TPU:1, one launch (start us, length us, event | category | flops | bytes accessed | tf_op | source)
XLA Modules:
  0.0 50.4 jit_solution(1872223168923859186)
XLA Ops:
  0.0 48.8 %shard_map.64 = bf16[12,2,32,128]{3,2,1,0:T(8,128)(2,1)} custom-call(s32[8,6]{1,0:T(8,128)} %domain_ref.1, s32[2,12]{1,0:T(2,128)} %bitcast.2, s32[2,12]{1,0:T(2,128)} %bitcast.3, bf16[64,112,256]{2,1,0:T(8,128)(2,1)} %panels_ref.1, bf16[12,2,256,128]{3,2,1,0:T(8,128)(2,1)} %d_ref.1, bf16[12,2,128,128]{3,2,1,0:T(8,128)(2,1)} %c_ref.1), custom_call_target="tpu_custom_call" | custom-call | tf_op jit(solution)/shard_map/pallas_call | solution.py:337
  48.8 1.6 %copy.8 = bf16[12,2,32,128]{3,2,1,0:T(8,128)(2,1)} copy(bf16[12,2,32,128]{3,2,1,0:T(8,128)(2,1)} %shard_map.64) | data formatting | bytes 393216

commit v2 on v1

--- a/solution.py
+++ b/solution.py
@@ -82,7 +82,7 @@
     n, m, domain_ref, slots_ref, ranks_ref, panels_ref, d_ref, c_ref, out_ref,
     panels, outgoing, recv, block, d_raw, d_mask, c_raw, acc, send_buf, landed, total,
     place_ref, rank_ref, perm_ref, mine_order, orders,
-    local_sem, send_sem, recv_sem, order_send, order_recv, part_send, part_recv,
+    local_sem, send_sem, recv_sem, order_sem, part_send, part_recv, from_below, from_above,
 ):
     me = lax.axis_index("pairs")
     mine = lax.axis_index("aux")
@@ -95,6 +95,7 @@
     strip = width // m
     sure = complete_after(slots, pairs)
     last = CORES - 1
+    early = sure[-2] - 1
 
     def device(k, dest):
         return peer_of(chip, k, chips) * CORES + dest
@@ -105,8 +106,15 @@
             if k:
                 pl.semaphore_signal(barrier, inc=1, device_id=(device(k, dest), mine), device_id_type=MESH)
     pl.semaphore_signal(barrier, inc=1, device_id=(chip * CORES + 1 - core, mine), device_id_type=MESH)
-    for offset in range(1, m):
-        pl.semaphore_signal(barrier, inc=1, device_id=(me, lax.rem(mine + offset, m)), device_id_type=MESH)
+
+    @pl.when(mine > 0)
+    def _():
+        pl.semaphore_signal(barrier, inc=1, device_id=(me, mine - 1), device_id_type=MESH)
+
+    @pl.when(mine < m - 1)
+    def _():
+        pl.semaphore_signal(barrier, inc=1, device_id=(me, mine + 1), device_id_type=MESH)
+
     panels_copy = pltpu.make_async_copy(panels_ref, panels, local_sem.at[0])
     panels_copy.start()
     d_copy = pltpu.make_async_copy(d_ref, d_raw, local_sem.at[1])
@@ -125,14 +133,15 @@
     for q in range(pairs):
         perm_ref[q] = sum(jnp.where(rank[pair] == q, pair, 0) for pair in range(pairs))
 
-    pl.semaphore_wait(barrier, n + m - 2)
-
-    def order_copy(peer, k, slot):
+    beside = jnp.where(mine > 0, 1, 0) + jnp.where(mine < m - 1, 1, 0)
+    pl.semaphore_wait(barrier, n - 1 + beside)
+
+    def order_copy(peer):
         return pltpu.make_async_remote_copy(
             src_ref=mine_order,
-            dst_ref=orders.at[slot],
-            send_sem=order_send.at[k],
-            recv_sem=order_recv.at[slot],
+            dst_ref=orders.at[chip],
+            send_sem=order_sem.at[0],
+            recv_sem=order_sem.at[1],
             device_id=(peer, mine),
             device_id_type=MESH,
         )
@@ -141,8 +150,8 @@
     def _():
         for k in range(1, chips):
             for dest in range(CORES):
-                order_copy(device(k, dest), k * CORES + dest, chip).start()
-        order_copy(chip * CORES, 0, chip).start()
+                order_copy(device(k, dest)).start()
+        order_copy(chip * CORES).start()
 
     panels_copy.wait()
 
@@ -150,8 +159,8 @@
         return pltpu.make_async_remote_copy(
             src_ref=outgoing.at[dest, k, spot],
             dst_ref=recv.at[spot, k * CORES + core],
-            send_sem=send_sem.at[dest, k, spot],
-            recv_sem=recv_sem.at[spot, k * CORES + core],
+            send_sem=send_sem,
+            recv_sem=recv_sem.at[spot],
             device_id=(device(k, dest), mine),
             device_id_type=MESH,
         )
@@ -183,13 +192,17 @@
     for dest in range(last):
         send_all(dest, lambda k, spot: spot)
 
-    for k in range(1, chips):
-        slot = peer_of(chip, k, chips)
-        order_copy(chip * CORES, 0, slot).wait_recv()
+    def orders_done(sem, count):
+        whole = orders.at[pl.ds(0, count)]
+        pltpu.make_async_copy(whole, whole, order_sem.at[sem]).wait()
 
     @pl.when(core != last)
     def _():
-        order_copy(chip * CORES, 0, chip).wait_recv()
+        orders_done(1, chips)
+
+    @pl.when(core == last)
+    def _():
+        orders_done(1, chips - 1)
 
     @pl.when(core == last)
     def _():
@@ -197,6 +210,24 @@
             orders[chip, 0, spot] = mine_order[0, spot]
 
     send_all(last, lambda k, spot: orders[peer_of(chip, k, chips), 0, spot])
+
+    for far in range(2, m):
+
+        @pl.when((mine >= far - 1) & (mine < m - 1))
+        def _():
+            pl.semaphore_signal(from_below, inc=1, device_id=(me, mine + 1), device_id_type=MESH)
+
+        @pl.when((mine <= m - far) & (mine > 0))
+        def _():
+            pl.semaphore_signal(from_above, inc=1, device_id=(me, mine - 1), device_id_type=MESH)
+
+        @pl.when(mine >= far)
+        def _():
+            pl.semaphore_wait(from_below, 1)
+
+        @pl.when(mine < m - far)
+        def _():
+            pl.semaphore_wait(from_above, 1)
 
     columns = lax.broadcasted_iota(jnp.int32, (1, width), 1)
     row_ids = lax.broadcasted_iota(jnp.int32, (width, 1), 0)
@@ -220,8 +251,8 @@
         return pltpu.make_async_remote_copy(
             src_ref=send_buf.at[peer, q],
             dst_ref=landed.at[offset - 1, q],
-            send_sem=part_send.at[q, offset],
-            recv_sem=part_recv.at[q, offset],
+            send_sem=part_send,
+            recv_sem=part_recv.at[jnp.maximum(q - early, 0)],
             device_id=(me, peer),
             device_id_type=MESH,
         )
@@ -255,26 +286,9 @@
         return carry
 
     def take(spot):
-        for lane in range(n):
-            if lane < CORES:
-
-                @pl.when(core != lane)
-                def _():
-                    arrived(lane, spot).wait_recv()
-
-            else:
-                arrived(lane, spot).wait_recv()
+        others = recv.at[spot, pl.ds(0, n - 1)]
+        pltpu.make_async_copy(others, others, recv_sem.at[spot]).wait()
         block[spot] = recv[spot].reshape(n * rows, nv)
-
-    def arrived(lane, spot):
-        return pltpu.make_async_remote_copy(
-            src_ref=outgoing.at[0, 0, spot],
-            dst_ref=recv.at[spot, lane],
-            send_sem=send_sem.at[0, 0, spot],
-            recv_sem=recv_sem.at[spot, lane],
-            device_id=(chip * CORES + 1 - core, mine),
-            device_id_type=MESH,
-        )
 
     @pl.when(core != last)
     def _():
@@ -292,36 +306,34 @@
             lax.fori_loop(done, sure[spot], compute, 0)
             done = sure[spot]
 
-    for q in range(pairs):
-        for offset in range(1, m):
-            part_copy(q, offset).wait_recv()
+    gone = outgoing.at[:, pl.ds(1, chips - 1)]
+    pltpu.make_async_copy(gone, gone, send_sem).wait()
+    gone = outgoing.at[0, 0]
+    pltpu.make_async_copy(gone, gone, send_sem).wait()
+
+    @pl.when(core == last)
+    def _():
+        for _ in range(n - 1):
+            orders_done(0, 1)
+
+    def sum_of(q):
         value = acc[q, :, pl.ds(pl.multiple_of(mine * strip, strip), strip), :]
         for offset in range(1, m):
             value = value + landed[offset - 1, q].astype(jnp.float32)
         total[q] = value.astype(total.dtype)
+
+    lots = landed.at[:, pl.ds(0, early + 1)]
+    pltpu.make_async_copy(lots, lots, part_recv.at[0]).wait()
+    for q in range(early + 1):
+        sum_of(q)
+    for q in range(early + 1, pairs):
+        lot = landed.at[:, q]
+        pltpu.make_async_copy(lot, lot, part_recv.at[q - early]).wait()
+        sum_of(q)
     for pair in range(pairs):
         out_ref[pair] = total[rank_ref[pair]]
-
-    for dest in range(CORES):
-        for spot in range(slots):
-            for k in range(1, chips):
-                panel_copy(k, dest, spot).wait_send()
-
-        @pl.when(core != dest)
-        def _():
-            for spot in range(slots):
-                panel_copy(0, dest, spot).wait_send()
-
-    @pl.when(core == last)
-    def _():
-        for k in range(1, chips):
-            for dest in range(CORES):
-                order_copy(device(k, dest), k * CORES + dest, chip).wait_send()
-        order_copy(chip * CORES, 0, chip).wait_send()
-
-    for q in range(pairs):
-        for offset in range(1, m):
-            part_copy(q, offset).wait_send()
+    sent = send_buf.at[pl.ds(0, m - 1)]
+    pltpu.make_async_copy(sent, sent, part_send).wait()
 
 
 def per_device(n, m, panels, domain, pair_slots, ranks, transforms, trial):
@@ -338,7 +350,7 @@
         functools.partial(fused_kernel, n, m),
         in_specs=[smem, smem, smem, hbm, hbm, hbm],
         out_specs=pl.BlockSpec(memory_space=pltpu.VMEM),
-        out_shape=jax.ShapeDtypeStruct((pairs, roots, strip, width), bf16),
+        out_shape=pltpu.VMEM((pairs, roots, strip, width), bf16),
         scratch_shapes=[
             pltpu.VMEM(panels.shape, bf16),
             pltpu.VMEM((CORES, chips, slots, rows, nv), bf16),
@@ -357,12 +369,13 @@
             pltpu.SMEM((1, 128), jnp.int32),
             pltpu.SMEM((chips, 1, 128), jnp.int32),
             dma((3,)),
-            dma((CORES, chips, slots)),
-            dma((slots, n)),
-            dma((n,)),
-            dma((chips,)),
-            dma((pairs, m)),
-            dma((pairs, m)),
+            dma,
+            dma((slots,)),
+            dma((2,)),
+            dma,
+            dma((pairs - complete_after(slots, pairs)[-2] + 1,)),
+            pltpu.SemaphoreType.REGULAR,
+            pltpu.SemaphoreType.REGULAR,
         ],
         compiler_params=pltpu.CompilerParams(
             collective_id=0, has_side_effects=True, vmem_limit_bytes=60 * 2**20

time: 50.6 us -> 47.2 us (0.933)
  Pallas kernels: 48.8 us -> 46.4 us
  local copies, waits for them, and re-layouts: 1.62 us -> 0.68 us
    pallas_call x1, Pallas kernels: 48.8 us -> 46.4 us  [per_device(): pl.pallas_call(functools.partial(fused_kernel, n, m), in_specs=[smem, sme...]
    unnamed x1, local copies, waits for them, and re-layouts: 1.62 us -> 0.68 us
where the time goes in v2:
time: 47.2 us; the launch traced here: 47.1 us
  Pallas kernels  46.4 us (98%)
  local copies, waits for them, and re-layouts  0.68 us (1%)
    pallas_call x1, Pallas kernels, per_device(): pl.pallas_call(functools.partial(fused_kernel, n, m), in_specs=[smem, sme...  46.4 us

profile of v2, /device:TPU:1, one launch (start us, length us, event | category | flops | bytes accessed | tf_op | source)
XLA Modules:
  0.0 47.1 jit_solution(17656657383212705395)
XLA Ops:
  0.0 46.4 %shard_map.64 = bf16[12,2,32,128]{3,2,1,0:T(8,128)(2,1)S(1)} custom-call(s32[8,6]{1,0:T(8,128)} %domain_ref.1, s32[2,12]{1,0:T(2,128)} %bitcast.2, s32[2,12]{1,0:T(2,128)} %bitcast.3, bf16[64,112,256]{2,1,0:T(8,128)(2,1)} %panels_ref.1, bf16[12,2,256,128]{3,2,1,0:T(8,128)(2,1)} %d_ref.1, bf16[12,2,128,128]{3,2,1,0:T(8,128)(2,1)} %c_ref.1), custom_call_target="tpu_custom_call" | custom-call | tf_op jit(solution)/shard_map/pallas_call | solution.py:349
  46.4 0.7 %copy.8 = bf16[12,2,32,128]{3,2,1,0:T(8,128)(2,1)} copy(bf16[12,2,32,128]{3,2,1,0:T(8,128)(2,1)S(1)} %shard_map.64) | data formatting | bytes 393216

commit v3 on v2

v3 whole, which is shorter than its diff:
```python
import functools

import jax
import jax.numpy as jnp
from jax import lax
from jax.experimental import pallas as pl
from jax.experimental.pallas import tpu as pltpu
from jax.sharding import PartitionSpec as P

MESH = pl.DeviceIdType.MESH
CORES = 2
BATCH = 4
FIXED = 2


def peer_of(me, offset, count):
    if count & (count - 1):
        return lax.rem(me + offset, count)
    peer = me
    bit = 1
    while bit < count:
        if offset & bit:
            peer = peer + bit * (1 - 2 * lax.rem(me // bit, 2))
        bit *= 2
    return peer


def complete_after(slots, pairs, fixed):
    sure = pairs
    counts = [pairs]
    for left in range(slots, 1, -1):
        sure -= min(sure, 2 * sure // (left - fixed)) if left > fixed else sure
        counts.insert(0, sure)
    return counts


def elimination(slots_ref, slots, pairs, fixed):
    bits = (pairs + 1).bit_length()
    left = [slots_ref[0, pair] for pair in range(pairs)]
    right = [slots_ref[1, pair] for pair in range(pairs)]
    fields = 31 // bits
    words = -(-slots // fields)

    def mark(slot, word):
        low = word * fields
        shift = slot - low
        inside = (shift >= 0) & (shift < fields)
        return jnp.where(inside, jnp.left_shift(1, jnp.where(inside, shift, 0) * bits), 0)

    marks = [[mark(left[p], w) | mark(right[p], w) for w in range(words)] for p in range(pairs)]
    alive = [jnp.int32(1)] * pairs
    rank = [jnp.int32(0)] * pairs
    place = [jnp.int32(0)] * slots
    taken = [jnp.int32(0)] * slots
    for spot in range(slots - 1, -1, -1):
        totals = [sum(alive[p] * marks[p][w] for p in range(pairs)) for w in range(words)]
        best, pick = None, None
        for slot in range(slots):
            count = (totals[slot // fields] >> (bits * (slot % fields))) & (2**bits - 1)
            count = count + (taken[slot] * (slots + 1) + jnp.maximum(fixed - slot, 0)) * 2**bits
            if best is None:
                best, pick = count, jnp.int32(slot)
            else:
                less = count < best
                best = jnp.where(less, count, best)
                pick = jnp.where(less, slot, pick)
        for slot in range(slots):
            hit = pick == slot
            place[slot] = jnp.where(hit, spot, place[slot])
            taken[slot] = jnp.where(hit, 1, taken[slot])
        gone = []
        for p in range(pairs):
            touch = (left[p] == pick) | (right[p] == pick)
            gone.append(jnp.where(touch, alive[p], 0))
            alive[p] = alive[p] - gone[p]
        at = sum(alive)
        for p in range(pairs):
            rank[p] = jnp.where(gone[p] == 1, at, rank[p])
            at = at + gone[p]
    return place, rank


def fused_kernel(
    n, m, domain_ref, slots_ref, ranks_ref, panels_ref, d_ref, c_ref, out_ref,
    panels, outgoing, recv, block, turned, d_raw, d_mask, d_turned, c_raw, c_pair, acc, send_buf, landed, total,
    place_ref, rank_ref, perm_ref, mine_order, landed_orders, orders,
    local_sem, send_sem, recv_sem, order_sem, part_send, part_recv, from_below, from_above,
):
    me = lax.axis_index("pairs")
    mine = lax.axis_index("aux")
    core = lax.rem(me, CORES)
    chip = me // CORES
    chips = n // CORES
    pairs, roots, nv, width = d_ref.shape
    slots = domain_ref.shape[1]
    rows = panels_ref.shape[1]
    strip = width // m
    early = complete_after(slots, pairs, 0)[-2] - 1

    def device(k, dest):
        return peer_of(chip, k, chips) * CORES + dest

    barrier = pltpu.get_barrier_semaphore()
    for k in range(chips):
        for dest in range(CORES):
            if k:
                pl.semaphore_signal(barrier, inc=1, device_id=(device(k, dest), mine), device_id_type=MESH)
    pl.semaphore_signal(barrier, inc=1, device_id=(chip * CORES + 1 - core, mine), device_id_type=MESH)

    @pl.when(mine > 0)
    def _():
        pl.semaphore_signal(barrier, inc=1, device_id=(me, mine - 1), device_id_type=MESH)

    @pl.when(mine < m - 1)
    def _():
        pl.semaphore_signal(barrier, inc=1, device_id=(me, mine + 1), device_id_type=MESH)

    panels_copy = pltpu.make_async_copy(panels_ref, panels, local_sem.at[0])
    panels_copy.start()
    d_copy = pltpu.make_async_copy(d_ref, d_raw, local_sem.at[1])
    d_copy.start()
    c_copy = pltpu.make_async_copy(c_ref, c_raw, local_sem.at[2])
    c_copy.start()

    place, rank = elimination(slots_ref, slots, pairs, jnp.where(core == 0, FIXED, 0))
    for slot in range(slots):
        place_ref[slot] = place[slot]
    for pair in range(pairs):
        rank_ref[pair] = rank[pair]
    lanes = lax.broadcasted_iota(jnp.int32, (1, 128), 1)
    own_order = []
    for spot in range(slots):
        chosen = sum(jnp.where(place[slot] == spot, slot, 0) for slot in range(slots))
        own_order.append(chosen)
    line = jnp.zeros((1, 128), jnp.int32)
    for spot in range(slots):
        line = jnp.where(lanes == spot, own_order[spot], line)
    mine_order[...] = line
    for q in range(pairs):
        perm_ref[q] = sum(jnp.where(rank[pair] == q, pair, 0) for pair in range(pairs))

    beside = jnp.where(mine > 0, 1, 0) + jnp.where(mine < m - 1, 1, 0)
    pl.semaphore_wait(barrier, n - 1 + beside)

    def order_copy(peer):
        return pltpu.make_async_remote_copy(
            src_ref=mine_order,
            dst_ref=landed_orders.at[me],
            send_sem=order_sem.at[0],
            recv_sem=order_sem.at[1],
            device_id=(peer, mine),
            device_id_type=MESH,
        )

    for k in range(1, chips):
        for dest in range(CORES):
            order_copy(device(k, dest)).start()
    order_copy(chip * CORES + 1 - core).start()

    panels_copy.wait()

    def panel_copy(k, dest, spot):
        return pltpu.make_async_remote_copy(
            src_ref=outgoing.at[dest, k, spot],
            dst_ref=recv.at[spot, k * CORES + core],
            send_sem=send_sem,
            recv_sem=recv_sem.at[spot],
            device_id=(device(k, dest), mine),
            device_id_type=MESH,
        )

    def gather(dest, k, spot, ordered=True):
        peer = device(k, dest)
        slot = orders[peer, 0, jnp.minimum(spot, slots - 1)] if ordered else spot
        outgoing[dest, k, spot] = panels[domain_ref[peer, slot]]

    def send_near(dest, spots, ordered=True):
        for spot in spots:
            gather(dest, 0, spot, ordered)

        @pl.when(core != dest)
        def _():
            for spot in spots:
                panel_copy(0, dest, spot).start()

        @pl.when(core == dest)
        def _():
            for spot in spots:
                recv[spot, dest] = outgoing[dest, 0, spot]

    def send_far(dest, spots, ordered=True):
        waiting = None
        for spot in spots:
            for k in range(1, chips):
                gather(dest, k, spot, ordered)
                if waiting is not None:
                    waiting.start()
                waiting = panel_copy(k, dest, spot)
        waiting.start()

    def send_led(dest):
        def spot_of(k, turn):
            ahead = peer_of(chip, k, chips) == 0
            spot = jnp.where(ahead, turn + 1, jnp.where(turn < 0, slots, turn))
            return spot, spot < slots

        def start(k, turn):
            spot, real = spot_of(k, turn)

            @pl.when(real)
            def _():
                panel_copy(k, dest, jnp.minimum(spot, slots - 1)).start()

        rounds = [(k, turn) for turn in range(-1, slots) for k in range(1, chips)]
        for index, (k, turn) in enumerate(rounds):
            gather(dest, k, spot_of(k, turn)[0])
            if index:
                start(*rounds[index - 1])
        start(*rounds[-1])

    def orders_done(sem):
        whole = landed_orders.at[pl.ds(0, n - 1)]
        pltpu.make_async_copy(whole, whole, order_sem.at[sem]).wait()

    send_far(0, range(FIXED), ordered=False)
    send_near(0, range(FIXED), ordered=False)
    landed_orders[me] = mine_order[...]
    orders_done(1)
    orders_copy = pltpu.make_async_copy(landed_orders, orders, local_sem.at[3])
    orders_copy.start()
    orders_copy.wait()
    send_far(0, range(FIXED, slots))
    for dest in range(1, CORES):
        send_led(dest)
        send_near(dest, range(slots))
    send_near(0, range(FIXED, slots))

    for far in range(2, m):

        @pl.when((mine >= far - 1) & (mine < m - 1))
        def _():
            pl.semaphore_signal(from_below, inc=1, device_id=(me, mine + 1), device_id_type=MESH)

        @pl.when((mine <= m - far) & (mine > 0))
        def _():
            pl.semaphore_signal(from_above, inc=1, device_id=(me, mine - 1), device_id_type=MESH)

        @pl.when(mine >= far)
        def _():
            pl.semaphore_wait(from_below, 1)

        @pl.when(mine < m - far)
        def _():
            pl.semaphore_wait(from_above, 1)

    columns = lax.broadcasted_iota(jnp.int32, (1, width), 1)
    row_ids = lax.broadcasted_iota(jnp.int32, (width, 1), 0)
    d_copy.wait()
    c_copy.wait()

    def mask_pair(pair, carry):
        for root in range(roots):
            limit = ranks_ref[root, pair]
            kept = jnp.where(columns < limit, d_raw[pair, root], jnp.zeros((), d_raw.dtype))
            d_mask[pair, :, root * width:(root + 1) * width] = kept
            d_turned[pair, root * width:(root + 1) * width] = kept.T
            keep = (columns < limit) & (row_ids < limit)
            kept = jnp.where(keep, c_raw[pair, root], jnp.zeros((), c_raw.dtype))
            c_pair[pair, root, :, :width] = kept
            c_pair[pair, root, :, width:] = kept.T
        return carry

    lax.fori_loop(0, pairs, mask_pair, 0)

    def part_copy(q, owner):
        return pltpu.make_async_remote_copy(
            src_ref=send_buf.at[owner, q],
            dst_ref=landed.at[mine, q],
            send_sem=part_send,
            recv_sem=part_recv.at[max(q - early, 0)],
            device_id=(me, owner),
            device_id_type=MESH,
        )

    def split(value):
        high = value.astype(jnp.bfloat16)
        return high, (value - high.astype(jnp.float32)).astype(jnp.bfloat16)

    def dot(left, right):
        return jnp.dot(left, right, preferred_element_type=jnp.float32)

    def compute(first, count):
        qs = [first + index for index in range(count)]
        which = [perm_ref[q] for q in qs]
        grams = [
            dot(turned[place_ref[slots_ref[0, pair]]], block[place_ref[slots_ref[1, pair]]]) for pair in which
        ]
        halves = []
        for gram, pair in zip(grams, which):
            both = dot(jnp.concatenate(split(gram), axis=0), d_mask[pair])
            halves.append(both[:nv] + both[nv:])
        wholes = []
        for half, pair in zip(halves, which):
            high, low = split(half)
            wholes.append(dot(d_turned[pair], high) + dot(d_turned[pair], low))
        kmats = [
            [whole[root * width:(root + 1) * width, root * width:(root + 1) * width] for root in range(roots)]
            for whole in wholes
        ]
        sides = [
            [dot(kmat[root].astype(jnp.bfloat16), c_pair[pair, root]) for root in range(roots)]
            for kmat, pair in zip(kmats, which)
        ]
        for q, kmat, side in zip(qs, kmats, sides):
            for root in range(roots):
                sigma = kmat[root] + side[root][:, :width] + side[root][:, width:].T
                acc[q, root] = sigma
                for owner in range(m):
                    send_buf[owner, q, root] = sigma[owner * strip:(owner + 1) * strip].astype(jnp.bfloat16)
        for owner in range(m):

            @pl.when(mine != owner)
            def _():
                for q in qs:
                    part_copy(q, owner).start()

    def take(spot):
        others = recv.at[spot, pl.ds(0, n - 1)]
        pltpu.make_async_copy(others, others, recv_sem.at[spot]).wait()
        whole = recv[spot].reshape(n * rows, nv)
        block[spot] = whole
        turned[spot] = whole.T

    def run(counts, spot):
        done = counts[spot - 1] if spot else 0
        while done < counts[spot]:
            step = min(BATCH, counts[spot] - done)
            compute(done, step)
            done += step

    for spot in range(slots):
        take(spot)

        @pl.when(core == 0)
        def _():
            run(complete_after(slots, pairs, FIXED), spot)

        @pl.when(core != 0)
        def _():
            run(complete_after(slots, pairs, 0), spot)

    gone = outgoing.at[:, pl.ds(1, chips - 1), pl.ds(0, slots)]
    pltpu.make_async_copy(gone, gone, send_sem).wait()
    gone = outgoing.at[0, 0, pl.ds(0, slots)]
    pltpu.make_async_copy(gone, gone, send_sem).wait()

    orders_done(0)

    def sum_of(q):
        value = acc[q, :, pl.ds(pl.multiple_of(mine * strip, strip), strip), :]
        for offset in range(1, m):
            value = value + landed[lax.rem(mine + offset, m), q].astype(jnp.float32)
        total[q] = value.astype(total.dtype)

    lots = landed.at[pl.ds(0, m - 1), pl.ds(0, early + 1)]
    pltpu.make_async_copy(lots, lots, part_recv.at[0]).wait()
    for q in range(early + 1):
        sum_of(q)
    for q in range(early + 1, pairs):
        lot = landed.at[pl.ds(0, m - 1), q]
        pltpu.make_async_copy(lot, lot, part_recv.at[q - early]).wait()
        sum_of(q)
    for pair in range(pairs):
        out_ref[pair] = total[rank_ref[pair]]
    sent = send_buf.at[pl.ds(0, m - 1)]
    pltpu.make_async_copy(sent, sent, part_send).wait()


def per_device(n, m, panels, domain, pair_slots, ranks, transforms, trial):
    pairs, roots, nv, width = transforms.shape
    slots = domain.shape[1]
    rows = panels.shape[1]
    chips = n // CORES
    strip = width // m
    bf16 = jnp.bfloat16
    smem = pl.BlockSpec(memory_space=pltpu.SMEM)
    hbm = pl.BlockSpec(memory_space=pltpu.HBM)
    dma = pltpu.SemaphoreType.DMA
    return pl.pallas_call(
        functools.partial(fused_kernel, n, m),
        in_specs=[smem, smem, smem, hbm, hbm, hbm],
        out_specs=pl.BlockSpec(memory_space=pltpu.VMEM),
        out_shape=pltpu.VMEM((pairs, roots, strip, width), bf16),
        scratch_shapes=[
            pltpu.VMEM(panels.shape, bf16),
            pltpu.VMEM((CORES, chips, slots + 1, rows, nv), bf16),
            pltpu.VMEM((slots, n, rows, nv), bf16),
            pltpu.VMEM((slots, n * rows, nv), bf16),
            pltpu.VMEM((slots, nv, n * rows), bf16),
            pltpu.VMEM((pairs, roots, nv, width), bf16),
            pltpu.VMEM((pairs, nv, roots * width), bf16),
            pltpu.VMEM((pairs, roots * width, nv), bf16),
            pltpu.VMEM((pairs, roots, width, width), bf16),
            pltpu.VMEM((pairs, roots, width, 2 * width), bf16),
            pltpu.VMEM((pairs, roots, width, width), jnp.float32),
            pltpu.VMEM((m, pairs, roots, strip, width), bf16),
            pltpu.VMEM((m, pairs, roots, strip, width), bf16),
            pltpu.VMEM((pairs, roots, strip, width), bf16),
            pltpu.SMEM((slots,), jnp.int32),
            pltpu.SMEM((pairs,), jnp.int32),
            pltpu.SMEM((pairs,), jnp.int32),
            pltpu.VMEM((1, 128), jnp.int32),
            pltpu.VMEM((n, 1, 128), jnp.int32),
            pltpu.SMEM((n, 1, 128), jnp.int32),
            dma((4,)),
            dma,
            dma((slots,)),
            dma((2,)),
            dma,
            dma((pairs - complete_after(slots, pairs, 0)[-2] + 1,)),
            pltpu.SemaphoreType.REGULAR,
            pltpu.SemaphoreType.REGULAR,
        ],
        compiler_params=pltpu.CompilerParams(
            collective_id=0, has_side_effects=True, vmem_limit_bytes=60 * 2**20
        ),
    )(domain, pair_slots.T, ranks.T, panels, transforms, trial)


def solution(mesh):
    return jax.shard_map(
        functools.partial(per_device, mesh.shape["pairs"], mesh.shape["aux"]),
        mesh=mesh,
        in_specs=(
            P(None, ("pairs", "aux"), None),
            P(),
            P("pairs", None),
            P("pairs", None),
            P("pairs", None, None, None),
            P("pairs", None, None, None),
        ),
        out_specs=P("pairs", None, "aux", None),
        check_vma=False,
    )
```

time: 47.2 us -> 43.7 us (0.926)
  Pallas kernels: 46.4 us -> 42.7 us
    pallas_call x1, Pallas kernels: 46.4 us -> 42.7 us  [per_device(): pl.pallas_call(functools.partial(fused_kernel, n, m), in_specs=[smem, sme...]
where the time goes in v3:
time: 43.7 us; the launch traced here: 43.4 us
  Pallas kernels  42.7 us (98%)
  local copies, waits for them, and re-layouts  0.68 us (2%)
    pallas_call x1, Pallas kernels, per_device(): pl.pallas_call(functools.partial(fused_kernel, n, m), in_specs=[smem, sme...  42.7 us

profile of v3, /device:TPU:1, one launch (start us, length us, event | category | flops | bytes accessed | tf_op | source)
XLA Modules:
  0.0 43.4 jit_solution(2742357129648288487)
XLA Ops:
  0.0 42.7 %shard_map.64 = bf16[12,2,32,128]{3,2,1,0:T(8,128)(2,1)S(1)} custom-call(s32[8,6]{1,0:T(8,128)} %domain_ref.1, s32[2,12]{1,0:T(2,128)} %bitcast.2, s32[2,12]{1,0:T(2,128)} %bitcast.3, bf16[64,112,256]{2,1,0:T(8,128)(2,1)} %panels_ref.1, bf16[12,2,256,128]{3,2,1,0:T(8,128)(2,1)} %d_ref.1, bf16[12,2,128,128]{3,2,1,0:T(8,128)(2,1)} %c_ref.1), custom_call_target="tpu_custom_call" | custom-call | tf_op jit(solution)/shard_map/pallas_call | solution.py:389
  42.7 0.7 %copy.8 = bf16[12,2,32,128]{3,2,1,0:T(8,128)(2,1)} copy(bf16[12,2,32,128]{3,2,1,0:T(8,128)(2,1)S(1)} %shard_map.64) | data formatting | bytes 393216

commit v4 on v3

--- a/solution.py
+++ b/solution.py
@@ -10,6 +10,7 @@
 MESH = pl.DeviceIdType.MESH
 CORES = 2
 BATCH = 4
+LATE = 4
 FIXED = 2
 
 
@@ -81,7 +82,8 @@
 
 
 def fused_kernel(
-    n, m, domain_ref, slots_ref, ranks_ref, panels_ref, d_ref, c_ref, out_ref,
+    n, m, domain_in, slots_in, ranks_in, panels_ref, d_ref, c_ref, out_ref,
+    domain_ref, slots_ref, ranks_ref,
     panels, outgoing, recv, block, turned, d_raw, d_mask, d_turned, c_raw, c_pair, acc, send_buf, landed, total,
     place_ref, rank_ref, perm_ref, mine_order, landed_orders, orders,
     local_sem, send_sem, recv_sem, order_sem, part_send, part_recv, from_below, from_above,
@@ -92,10 +94,14 @@
     chip = me // CORES
     chips = n // CORES
     pairs, roots, nv, width = d_ref.shape
-    slots = domain_ref.shape[1]
+    slots = domain_in.shape[1]
     rows = panels_ref.shape[1]
     strip = width // m
-    early = complete_after(slots, pairs, 0)[-2] - 1
+    early = complete_after(slots, pairs, 0)[-2]
+
+    def group_of(q):
+        return 0 if q < early else 1 + (q - early) // LATE
+
 
     def device(k, dest):
         return peer_of(chip, k, chips) * CORES + dest
@@ -115,6 +121,14 @@
     def _():
         pl.semaphore_signal(barrier, inc=1, device_id=(me, mine + 1), device_id_type=MESH)
 
+    small = [
+        pltpu.make_async_copy(source, target, local_sem.at[4 + index])
+        for index, (source, target) in enumerate(
+            [(slots_in, slots_ref), (domain_in, domain_ref), (ranks_in, ranks_ref)]
+        )
+    ]
+    for copy in small:
+        copy.start()
     panels_copy = pltpu.make_async_copy(panels_ref, panels, local_sem.at[0])
     panels_copy.start()
     d_copy = pltpu.make_async_copy(d_ref, d_raw, local_sem.at[1])
@@ -122,6 +136,8 @@
     c_copy = pltpu.make_async_copy(c_ref, c_raw, local_sem.at[2])
     c_copy.start()
 
+    for copy in small:
+        copy.wait()
     place, rank = elimination(slots_ref, slots, pairs, jnp.where(core == 0, FIXED, 0))
     for slot in range(slots):
         place_ref[slot] = place[slot]
@@ -277,7 +293,7 @@
             src_ref=send_buf.at[owner, q],
             dst_ref=landed.at[mine, q],
             send_sem=part_send,
-            recv_sem=part_recv.at[max(q - early, 0)],
+            recv_sem=part_recv.at[group_of(q)],
             device_id=(me, owner),
             device_id_type=MESH,
         )
@@ -334,7 +350,8 @@
     def run(counts, spot):
         done = counts[spot - 1] if spot else 0
         while done < counts[spot]:
-            step = min(BATCH, counts[spot] - done)
+            limit = min(BATCH, early - done) if done < early else LATE - (done - early) % LATE
+            step = min(limit, counts[spot] - done)
             compute(done, step)
             done += step
 
@@ -356,20 +373,15 @@
 
     orders_done(0)
 
-    def sum_of(q):
-        value = acc[q, :, pl.ds(pl.multiple_of(mine * strip, strip), strip), :]
+    edges = [0, *range(early, pairs, LATE), pairs]
+    for group, (low, high) in enumerate(zip(edges, edges[1:])):
+        part = pl.ds(low, high - low)
+        lot = landed.at[pl.ds(0, m - 1), part]
+        pltpu.make_async_copy(lot, lot, part_recv.at[group]).wait()
+        value = acc[part, :, pl.ds(pl.multiple_of(mine * strip, strip), strip), :]
         for offset in range(1, m):
-            value = value + landed[lax.rem(mine + offset, m), q].astype(jnp.float32)
-        total[q] = value.astype(total.dtype)
-
-    lots = landed.at[pl.ds(0, m - 1), pl.ds(0, early + 1)]
-    pltpu.make_async_copy(lots, lots, part_recv.at[0]).wait()
-    for q in range(early + 1):
-        sum_of(q)
-    for q in range(early + 1, pairs):
-        lot = landed.at[pl.ds(0, m - 1), q]
-        pltpu.make_async_copy(lot, lot, part_recv.at[q - early]).wait()
-        sum_of(q)
+            value = value + landed[lax.rem(mine + offset, m), part].astype(jnp.float32)
+        total[part] = value.astype(total.dtype)
     for pair in range(pairs):
         out_ref[pair] = total[rank_ref[pair]]
     sent = send_buf.at[pl.ds(0, m - 1)]
@@ -383,15 +395,17 @@
     chips = n // CORES
     strip = width // m
     bf16 = jnp.bfloat16
-    smem = pl.BlockSpec(memory_space=pltpu.SMEM)
     hbm = pl.BlockSpec(memory_space=pltpu.HBM)
     dma = pltpu.SemaphoreType.DMA
     return pl.pallas_call(
         functools.partial(fused_kernel, n, m),
-        in_specs=[smem, smem, smem, hbm, hbm, hbm],
+        in_specs=[hbm] * 6,
         out_specs=pl.BlockSpec(memory_space=pltpu.VMEM),
         out_shape=pltpu.VMEM((pairs, roots, strip, width), bf16),
         scratch_shapes=[
+            pltpu.SMEM(domain.shape, jnp.int32),
+            pltpu.SMEM(pair_slots.shape[::-1], jnp.int32),
+            pltpu.SMEM(ranks.shape[::-1], jnp.int32),
             pltpu.VMEM(panels.shape, bf16),
             pltpu.VMEM((CORES, chips, slots + 1, rows, nv), bf16),
             pltpu.VMEM((slots, n, rows, nv), bf16),
@@ -412,12 +426,12 @@
             pltpu.VMEM((1, 128), jnp.int32),
             pltpu.VMEM((n, 1, 128), jnp.int32),
             pltpu.SMEM((n, 1, 128), jnp.int32),
-            dma((4,)),
+            dma((7,)),
             dma,
             dma((slots,)),
             dma((2,)),
             dma,
-            dma((pairs - complete_after(slots, pairs, 0)[-2] + 1,)),
+            dma((1 - (complete_after(slots, pairs, 0)[-2] - pairs) // LATE,)),
             pltpu.SemaphoreType.REGULAR,
             pltpu.SemaphoreType.REGULAR,
         ],

time: 43.7 us -> 42.8 us (0.979)
  Pallas kernels: 42.7 us -> 41.9 us
    pallas_call x1, Pallas kernels: 42.7 us -> 41.9 us  [per_device(): pl.pallas_call(functools.partial(fused_kernel, n, m), in_specs=[hbm] * 6,...]
where the time goes in v4:
time: 42.8 us; the launch traced here: 42.5 us
  Pallas kernels  41.9 us (98%)
  local copies, waits for them, and re-layouts  0.68 us (2%)
    pallas_call x1, Pallas kernels, per_device(): pl.pallas_call(functools.partial(fused_kernel, n, m), in_specs=[hbm] * 6,...  41.9 us

profile of v4, /device:TPU:1, one launch (start us, length us, event | category | flops | bytes accessed | tf_op | source)
XLA Modules:
  0.0 42.5 jit_solution(5448019875157875368)
XLA Ops:
  0.0 41.9 %shard_map.64 = bf16[12,2,32,128]{3,2,1,0:T(8,128)(2,1)S(1)} custom-call(s32[8,6]{1,0:T(8,128)} %domain_in.1, s32[2,12]{1,0:T(2,128)} %bitcast.2, s32[2,12]{1,0:T(2,128)} %bitcast.3, bf16[64,112,256]{2,1,0:T(8,128)(2,1)} %panels_ref.1, bf16[12,2,256,128]{3,2,1,0:T(8,128)(2,1)} %d_ref.1, bf16[12,2,128,128]{3,2,1,0:T(8,128)(2,1)} %c_ref.1), custom_call_target="tpu_custom_call" | custom-call | tf_op jit(solution)/shard_map/pallas_call | solution.py:400
  41.9 0.7 %copy.8 = bf16[12,2,32,128]{3,2,1,0:T(8,128)(2,1)} copy(bf16[12,2,32,128]{3,2,1,0:T(8,128)(2,1)S(1)} %shard_map.64) | data formatting | bytes 393216

commit v5 on v4

--- a/solution.py
+++ b/solution.py
@@ -103,6 +103,8 @@
         return 0 if q < early else 1 + (q - early) // LATE
 
 
+    around = sorted(range(1, chips), key=lambda k: -k.bit_count())
+
     def device(k, dest):
         return peer_of(chip, k, chips) * CORES + dest
 
@@ -187,7 +189,7 @@
 
     def gather(dest, k, spot, ordered=True):
         peer = device(k, dest)
-        slot = orders[peer, 0, jnp.minimum(spot, slots - 1)] if ordered else spot
+        slot = orders[peer, 0, spot] if ordered else spot
         outgoing[dest, k, spot] = panels[domain_ref[peer, slot]]
 
     def send_near(dest, spots, ordered=True):
@@ -207,32 +209,12 @@
     def send_far(dest, spots, ordered=True):
         waiting = None
         for spot in spots:
-            for k in range(1, chips):
+            for k in around:
                 gather(dest, k, spot, ordered)
                 if waiting is not None:
                     waiting.start()
                 waiting = panel_copy(k, dest, spot)
         waiting.start()
-
-    def send_led(dest):
-        def spot_of(k, turn):
-            ahead = peer_of(chip, k, chips) == 0
-            spot = jnp.where(ahead, turn + 1, jnp.where(turn < 0, slots, turn))
-            return spot, spot < slots
-
-        def start(k, turn):
-            spot, real = spot_of(k, turn)
-
-            @pl.when(real)
-            def _():
-                panel_copy(k, dest, jnp.minimum(spot, slots - 1)).start()
-
-        rounds = [(k, turn) for turn in range(-1, slots) for k in range(1, chips)]
-        for index, (k, turn) in enumerate(rounds):
-            gather(dest, k, spot_of(k, turn)[0])
-            if index:
-                start(*rounds[index - 1])
-        start(*rounds[-1])
 
     def orders_done(sem):
         whole = landed_orders.at[pl.ds(0, n - 1)]
@@ -247,7 +229,7 @@
     orders_copy.wait()
     send_far(0, range(FIXED, slots))
     for dest in range(1, CORES):
-        send_led(dest)
+        send_far(dest, range(slots))
         send_near(dest, range(slots))
     send_near(0, range(FIXED, slots))
 
@@ -327,17 +309,19 @@
             [dot(kmat[root].astype(jnp.bfloat16), c_pair[pair, root]) for root in range(roots)]
             for kmat, pair in zip(kmats, which)
         ]
-        for q, kmat, side in zip(qs, kmats, sides):
-            for root in range(roots):
-                sigma = kmat[root] + side[root][:, :width] + side[root][:, width:].T
-                acc[q, root] = sigma
-                for owner in range(m):
-                    send_buf[owner, q, root] = sigma[owner * strip:(owner + 1) * strip].astype(jnp.bfloat16)
-        for owner in range(m):
-
-            @pl.when(mine != owner)
-            def _():
-                for q in qs:
+        half = count
+        for low in range(0, count, half):
+            for at in range(low, min(low + half, count)):
+                q = qs[at]
+                for root in range(roots):
+                    side = sides[at][root]
+                    sigma = kmats[at][root] + side[:, :width] + side[:, width:].T
+                    acc[q, root] = sigma
+                    for owner in range(m):
+                        send_buf[owner, q, root] = sigma[owner * strip:(owner + 1) * strip].astype(jnp.bfloat16)
+            for turn in range(m - 1):
+                owner = turn + jnp.where(mine <= turn, 1, 0)
+                for q in qs[low:low + half]:
                     part_copy(q, owner).start()
 
     def take(spot):
@@ -366,9 +350,9 @@
         def _():
             run(complete_after(slots, pairs, 0), spot)
 
-    gone = outgoing.at[:, pl.ds(1, chips - 1), pl.ds(0, slots)]
+    gone = outgoing.at[:, pl.ds(1, chips - 1)]
     pltpu.make_async_copy(gone, gone, send_sem).wait()
-    gone = outgoing.at[0, 0, pl.ds(0, slots)]
+    gone = outgoing.at[0, 0]
     pltpu.make_async_copy(gone, gone, send_sem).wait()
 
     orders_done(0)
@@ -407,7 +391,7 @@
             pltpu.SMEM(pair_slots.shape[::-1], jnp.int32),
             pltpu.SMEM(ranks.shape[::-1], jnp.int32),
             pltpu.VMEM(panels.shape, bf16),
-            pltpu.VMEM((CORES, chips, slots + 1, rows, nv), bf16),
+            pltpu.VMEM((CORES, chips, slots, rows, nv), bf16),
             pltpu.VMEM((slots, n, rows, nv), bf16),
             pltpu.VMEM((slots, n * rows, nv), bf16),
             pltpu.VMEM((slots, nv, n * rows), bf16),

time: 42.8 us -> 42.7 us (level)
  no operation moved by 1% of the time
where the time goes in v5:
time: 42.7 us; the launch traced here: 42.5 us
  Pallas kernels  41.9 us (98%)
  local copies, waits for them, and re-layouts  0.68 us (2%)
    pallas_call x1, Pallas kernels, per_device(): pl.pallas_call(functools.partial(fused_kernel, n, m), in_specs=[hbm] * 6,...  41.9 us

profile of v5, /device:TPU:1, one launch (start us, length us, event | category | flops | bytes accessed | tf_op | source)
XLA Modules:
  0.0 42.5 jit_solution(10373812778153787611)
XLA Ops:
  0.0 41.9 %shard_map.64 = bf16[12,2,32,128]{3,2,1,0:T(8,128)(2,1)S(1)} custom-call(s32[8,6]{1,0:T(8,128)} %domain_in.1, s32[2,12]{1,0:T(2,128)} %bitcast.2, s32[2,12]{1,0:T(2,128)} %bitcast.3, bf16[64,112,256]{2,1,0:T(8,128)(2,1)} %panels_ref.1, bf16[12,2,256,128]{3,2,1,0:T(8,128)(2,1)} %d_ref.1, bf16[12,2,128,128]{3,2,1,0:T(8,128)(2,1)} %c_ref.1), custom_call_target="tpu_custom_call" | custom-call | tf_op jit(solution)/shard_map/pallas_call | solution.py:384
  41.9 0.7 %copy.8 = bf16[12,2,32,128]{3,2,1,0:T(8,128)(2,1)} copy(bf16[12,2,32,128]{3,2,1,0:T(8,128)(2,1)S(1)} %shard_map.64) | data formatting | bytes 393216

commit v6 on v5

--- a/solution.py
+++ b/solution.py
@@ -37,30 +37,30 @@
 
 def elimination(slots_ref, slots, pairs, fixed):
     bits = (pairs + 1).bit_length()
-    left = [slots_ref[0, pair] for pair in range(pairs)]
-    right = [slots_ref[1, pair] for pair in range(pairs)]
     fields = 31 // bits
     words = -(-slots // fields)
 
+    def shift_of(slot, word):
+        shift = slot - word * fields
+        inside = (shift >= 0) & (shift < fields) if words > 1 else True
+        return jnp.where(inside, shift, 0) * bits, inside
+
     def mark(slot, word):
-        low = word * fields
-        shift = slot - low
-        inside = (shift >= 0) & (shift < fields)
-        return jnp.where(inside, jnp.left_shift(1, jnp.where(inside, shift, 0) * bits), 0)
-
-    marks = [[mark(left[p], w) | mark(right[p], w) for w in range(words)] for p in range(pairs)]
-    alive = [jnp.int32(1)] * pairs
-    rank = [jnp.int32(0)] * pairs
+        shift, inside = shift_of(slot, word)
+        return jnp.where(inside, jnp.left_shift(1, shift), 0)
+
+    marks = [
+        [mark(slots_ref[0, p], w) | mark(slots_ref[1, p], w) for w in range(words)] for p in range(pairs)
+    ]
     place = [jnp.int32(0)] * slots
-    taken = [jnp.int32(0)] * slots
-    for spot in range(slots - 1, -1, -1):
-        totals = [sum(alive[p] * marks[p][w] for p in range(pairs)) for w in range(words)]
-        best, pick = None, None
+    extra = [jnp.maximum(fixed - slot, 0) * 2**bits for slot in range(slots)]
+    for spot in range(slots - 1, 0, -1):
+        totals = [sum(marks[p][w] for p in range(pairs)) for w in range(words)]
+        best, pick = None, jnp.int32(0)
         for slot in range(slots):
-            count = (totals[slot // fields] >> (bits * (slot % fields))) & (2**bits - 1)
-            count = count + (taken[slot] * (slots + 1) + jnp.maximum(fixed - slot, 0)) * 2**bits
+            count = ((totals[slot // fields] >> (bits * (slot % fields))) & (2**bits - 1)) + extra[slot]
             if best is None:
-                best, pick = count, jnp.int32(slot)
+                best = count
             else:
                 less = count < best
                 best = jnp.where(less, count, best)
@@ -68,17 +68,24 @@
         for slot in range(slots):
             hit = pick == slot
             place[slot] = jnp.where(hit, spot, place[slot])
-            taken[slot] = jnp.where(hit, 1, taken[slot])
-        gone = []
+            extra[slot] = jnp.where(hit, (slots + 1) * 2**bits, extra[slot])
         for p in range(pairs):
-            touch = (left[p] == pick) | (right[p] == pick)
-            gone.append(jnp.where(touch, alive[p], 0))
-            alive[p] = alive[p] - gone[p]
-        at = sum(alive)
-        for p in range(pairs):
-            rank[p] = jnp.where(gone[p] == 1, at, rank[p])
-            at = at + gone[p]
-    return place, rank
+            gone = 0
+            for w in range(words):
+                shift, inside = shift_of(pick, w)
+                gone = gone | jnp.where(inside, (marks[p][w] >> shift) & 1, 0)
+            marks[p] = [value & (gone - 1) for value in marks[p]]
+    return place
+
+
+def ranking(stages):
+    rank = [jnp.int32(0)] * len(stages)
+    for p in range(len(stages)):
+        for q in range(p + 1, len(stages)):
+            later = jnp.where(stages[p] > stages[q], 1, 0)
+            rank[p] = rank[p] + later
+            rank[q] = rank[q] + 1 - later
+    return rank
 
 
 def fused_kernel(
@@ -140,11 +147,9 @@
 
     for copy in small:
         copy.wait()
-    place, rank = elimination(slots_ref, slots, pairs, jnp.where(core == 0, FIXED, 0))
+    place = elimination(slots_ref, slots, pairs, jnp.where(core == 0, FIXED, 0))
     for slot in range(slots):
         place_ref[slot] = place[slot]
-    for pair in range(pairs):
-        rank_ref[pair] = rank[pair]
     lanes = lax.broadcasted_iota(jnp.int32, (1, 128), 1)
     own_order = []
     for spot in range(slots):
@@ -154,9 +159,6 @@
     for spot in range(slots):
         line = jnp.where(lanes == spot, own_order[spot], line)
     mine_order[...] = line
-    for q in range(pairs):
-        perm_ref[q] = sum(jnp.where(rank[pair] == q, pair, 0) for pair in range(pairs))
-
     beside = jnp.where(mine > 0, 1, 0) + jnp.where(mine < m - 1, 1, 0)
     pl.semaphore_wait(barrier, n - 1 + beside)
 
@@ -232,6 +234,17 @@
         send_far(dest, range(slots))
         send_near(dest, range(slots))
     send_near(0, range(FIXED, slots))
+
+    rank = ranking(
+        [
+            jnp.maximum(place_ref[slots_ref[0, pair]], place_ref[slots_ref[1, pair]])
+            for pair in range(pairs)
+        ]
+    )
+    for pair in range(pairs):
+        rank_ref[pair] = rank[pair]
+    for q in range(pairs):
+        perm_ref[q] = sum(jnp.where(rank[pair] == q, pair, 0) for pair in range(pairs))
 
     for far in range(2, m):
 
@@ -309,20 +322,16 @@
             [dot(kmat[root].astype(jnp.bfloat16), c_pair[pair, root]) for root in range(roots)]
             for kmat, pair in zip(kmats, which)
         ]
-        half = count
-        for low in range(0, count, half):
-            for at in range(low, min(low + half, count)):
-                q = qs[at]
-                for root in range(roots):
-                    side = sides[at][root]
-                    sigma = kmats[at][root] + side[:, :width] + side[:, width:].T
-                    acc[q, root] = sigma
-                    for owner in range(m):
-                        send_buf[owner, q, root] = sigma[owner * strip:(owner + 1) * strip].astype(jnp.bfloat16)
-            for turn in range(m - 1):
-                owner = turn + jnp.where(mine <= turn, 1, 0)
-                for q in qs[low:low + half]:
-                    part_copy(q, owner).start()
+        for q, kmat, side in zip(qs, kmats, sides):
+            for root in range(roots):
+                sigma = kmat[root] + side[root][:, :width] + side[root][:, width:].T
+                acc[q, root] = sigma
+                for owner in range(m):
+                    send_buf[owner, q, root] = sigma[owner * strip:(owner + 1) * strip].astype(jnp.bfloat16)
+        for turn in range(m - 1):
+            owner = turn + jnp.where(mine <= turn, 1, 0)
+            for q in qs:
+                part_copy(q, owner).start()
 
     def take(spot):
         others = recv.at[spot, pl.ds(0, n - 1)]

time: 42.7 us -> 42.7 us (level)
  no operation moved by 1% of the time
where the time goes in v6:
time: 42.7 us; the launch traced here: 42.5 us
  Pallas kernels  41.8 us (98%)
  local copies, waits for them, and re-layouts  0.68 us (2%)
    pallas_call x1, Pallas kernels, per_device(): pl.pallas_call(functools.partial(fused_kernel, n, m), in_specs=[hbm] * 6,...  41.8 us

profile of v6, /device:TPU:1, one launch (start us, length us, event | category | flops | bytes accessed | tf_op | source)
XLA Modules:
  0.0 42.5 jit_solution(2375972978657619177)
XLA Ops:
  0.0 41.8 %shard_map.64 = bf16[12,2,32,128]{3,2,1,0:T(8,128)(2,1)S(1)} custom-call(s32[8,6]{1,0:T(8,128)} %domain_in.1, s32[2,12]{1,0:T(2,128)} %bitcast.2, s32[2,12]{1,0:T(2,128)} %bitcast.3, bf16[64,112,256]{2,1,0:T(8,128)(2,1)} %panels_ref.1, bf16[12,2,256,128]{3,2,1,0:T(8,128)(2,1)} %d_ref.1, bf16[12,2,128,128]{3,2,1,0:T(8,128)(2,1)} %c_ref.1), custom_call_target="tpu_custom_call" | custom-call | tf_op jit(solution)/shard_map/pallas_call | solution.py:393
  41.8 0.7 %copy.8 = bf16[12,2,32,128]{3,2,1,0:T(8,128)(2,1)} copy(bf16[12,2,32,128]{3,2,1,0:T(8,128)(2,1)S(1)} %shard_map.64) | data formatting | bytes 393216
